TPU v7x, 16 devices: a whole 2x2x2 slice. The times are simulated.
16 devices in a mesh: data: 4 (over z, y), stage: 4 (over x, core).
Axes of the slice: x: 2, y: 2, z: 2, core: 2. Of those that a mesh axis runs over, the one named last changes fastest.
Arguments:
- X: bfloat16 [16, 512, 1536], P('data'), parts along dimension 0
- G: bfloat16 [16, 512, 1536], P('data'), parts along dimension 0
- W1: bfloat16 [4, 1536, 6144], P('stage')
- W2: bfloat16 [4, 6144, 1536], P('stage')
Outputs:
- output 1: bfloat16 [16, 512, 1536], P('data'), parts along dimension 0
- output 2: bfloat16 [16, 512, 1536], P('data'), parts along dimension 0
- output 3: float32 [16, 1536, 6144], P(('data', 'stage')), parts along dimension 0
- output 4: float32 [16, 6144, 1536], P(('data', 'stage')), parts along dimension 0
There are 4 independent parts. A program takes and returns all parts, laid end to end along the dimension named above; an argument that names none is the same for every part.
All inputs are finite; a program needn't handle non-finite values.
Results may differ from a plain program's by a relative error of at most 0.00963606.
Values are sent between devices in bfloat16 or wider.
A program may use at most 1 GiB of HBM per device.

v0:
```python
import jax
import jax.numpy as jnp
from jax import lax
from jax.sharding import PartitionSpec as P


def _fwd_layer(h, w1, w2):
    z = jnp.dot(h, w1, preferred_element_type=jnp.float32)
    u = jax.nn.gelu(z, approximate=True).astype(jnp.bfloat16)
    return (h.astype(jnp.float32) + jnp.dot(u, w2, preferred_element_type=jnp.float32)).astype(jnp.bfloat16)


def _bwd_layer(h, g, w1, w2):
    z = jnp.dot(h, w1, preferred_element_type=jnp.float32)
    u, gelu_vjp = jax.vjp(lambda t: jax.nn.gelu(t, approximate=True), z)
    du = jnp.dot(g, w2.T, preferred_element_type=jnp.float32)
    dz = gelu_vjp(du)[0].astype(jnp.bfloat16)
    dw2 = jnp.dot(u.astype(jnp.bfloat16).T, g, preferred_element_type=jnp.float32)
    dw1 = jnp.dot(h.T, dz, preferred_element_type=jnp.float32)
    dh = (g.astype(jnp.float32) + jnp.dot(dz, w1.T, preferred_element_type=jnp.float32)).astype(jnp.bfloat16)
    return dh, dw1, dw2


def _put(buf, i, val, ok):
    old = lax.dynamic_index_in_dim(buf, i, 0, keepdims=False)
    return lax.dynamic_update_index_in_dim(buf, jnp.where(ok, val, old), i, 0)


def solution(mesh):
    n_st = mesh.shape['stage']
    fwd_perm = [(i, i + 1) for i in range(n_st - 1)]
    bwd_perm = [(i + 1, i) for i in range(n_st - 1)]

    def body(x, g, w1, w2):
        s = lax.axis_index('stage')
        n_mb = x.shape[0]
        lps = w1.shape[0]
        first = s == 0
        last = s == n_st - 1
        ticks = n_mb + n_st - 1
        mb_shape = x.shape[1:]

        def fwd_tick(t, carry):
            recv, saved, y = carry
            m = t - s
            ok = (m >= 0) & (m < n_mb)
            mc = jnp.clip(m, 0, n_mb - 1)
            h = jnp.where(first, lax.dynamic_index_in_dim(x, mc, 0, keepdims=False), recv)
            hs = []
            for j in range(lps):
                hs.append(h)
                h = _fwd_layer(h, w1[j], w2[j])
            saved = _put(saved, mc, jnp.stack(hs), ok)
            y = _put(y, mc, h, ok & last)
            recv = lax.ppermute(h, 'stage', fwd_perm)
            return recv, saved, y

        recv0 = jnp.zeros(mb_shape, x.dtype)
        saved0 = jnp.zeros((n_mb, lps) + mb_shape, x.dtype)
        _, saved, y = lax.fori_loop(0, ticks, fwd_tick, (recv0, saved0, jnp.zeros_like(x)))

        def bwd_tick(t, carry):
            recv, dx, a1, a2 = carry
            m = t - (n_st - 1 - s)
            ok = (m >= 0) & (m < n_mb)
            mc = jnp.clip(m, 0, n_mb - 1)
            gh = jnp.where(last, lax.dynamic_index_in_dim(g, mc, 0, keepdims=False), recv)
            hs = lax.dynamic_index_in_dim(saved, mc, 0, keepdims=False)
            a1 = list(a1)
            a2 = list(a2)
            for j in reversed(range(lps)):
                gh, dw1, dw2 = _bwd_layer(hs[j], gh, w1[j], w2[j])
                a1[j] = a1[j] + jnp.where(ok, dw1, 0.0)
                a2[j] = a2[j] + jnp.where(ok, dw2, 0.0)
            dx = _put(dx, mc, gh, ok & first)
            recv = lax.ppermute(gh, 'stage', bwd_perm)
            return recv, dx, tuple(a1), tuple(a2)

        a10 = tuple(jnp.zeros(w1.shape[1:], jnp.float32) for _ in range(lps))
        a20 = tuple(jnp.zeros(w2.shape[1:], jnp.float32) for _ in range(lps))
        _, dx, a1, a2 = lax.fori_loop(0, ticks, bwd_tick, (recv0, jnp.zeros_like(x), a10, a20))
        y = lax.psum(y, 'stage')
        dx = lax.psum(dx, 'stage')
        return y, dx, jnp.stack(a1), jnp.stack(a2)

    return jax.shard_map(body, mesh=mesh,
                         in_specs=(P('data'), P('data'), P('stage'), P('stage')),
                         out_specs=(P('data'), P('data'), P(('data', 'stage')), P(('data', 'stage'))),
                         check_vma=False)
```

profile of v0, /device:TPU:0, one launch (start us, length us, event | category | flops | bytes accessed | tf_op | source)
XLA Modules:
  0.0 1508.7 jit_solution(13582891542209935115)
XLA Ops:
  13.7 371.3 %while.39 = (s32[]{:T(128)}, bf16[512,1536]{1,0:T(8,128)(2,1)S(1)}, bf16[4,1,512,1536]{3,2,1,0:T(8,128)(2,1)}, bf16[4,512,1536]{2,1,0:T(8,128)(2,1)}, pred[]{:T(...) while((s32[]{:T(128)}, bf16[512,1536]{1,0:T(8,128)(2,1)S(1)}, ...), condition=%wide.region_1.2_spmd, body=%wide.region_0.1_spmd.sunk | while | flops 19361955840 | bytes 70782200 | solution.py:60
  15.2 31.7 %bitcast_dynamic-update-slice_fusion.6 = (bf16[4,512,1536]{2,1,0:T(8,128)(2,1)}, bf16[512,1536]{1,0:T(8,128)(2,1)}) fusion(bf16[4,512,1536]{2,1,0:T(8,128)(2,1)} %get-tuple-element.717, s32[]{:T(128)S(6)} %min.21, bf16[1,512,1536]{2,1,0:T(8,128)(2,1)S(1)} %constant_dynamic-slice_fusion.6, pred[]{:T(512)S(6)} %and.42, ...), kind=kOutput, calls=%fused_computation.15.clone.1 | convolution fusion | flops 19360382976 | bytes 48761344 | tf_op jit(solution)/shard_map/while/body/eval_jaxpr/dot_general | solution.py:10
  56.0 31.8 %bitcast_dynamic-update-slice_fusion.6 = (bf16[4,512,1536]{2,1,0:T(8,128)(2,1)}, bf16[512,1536]{1,0:T(8,128)(2,1)}) fusion(bf16[4,512,1536]{2,1,0:T(8,128)(2,1)} %get-tuple-element.717, s32[]{:T(128)S(6)} %min.21, bf16[1,512,1536]{2,1,0:T(8,128)(2,1)S(1)} %constant_dynamic-slice_fusion.6, pred[]{:T(512)S(6)} %and.42, ...), kind=kOutput, calls=%fused_computation.15.clone.1 | convolution fusion | flops 19360382976 | bytes 48761344 | tf_op jit(solution)/shard_map/while/body/eval_jaxpr/dot_general | solution.py:10
  111.1 31.7 %bitcast_dynamic-update-slice_fusion.6 = (bf16[4,512,1536]{2,1,0:T(8,128)(2,1)}, bf16[512,1536]{1,0:T(8,128)(2,1)}) fusion(bf16[4,512,1536]{2,1,0:T(8,128)(2,1)} %get-tuple-element.717, s32[]{:T(128)S(6)} %min.21, bf16[1,512,1536]{2,1,0:T(8,128)(2,1)S(1)} %constant_dynamic-slice_fusion.6, pred[]{:T(512)S(6)} %and.42, ...), kind=kOutput, calls=%fused_computation.15.clone.1 | convolution fusion | flops 19360382976 | bytes 48761344 | tf_op jit(solution)/shard_map/while/body/eval_jaxpr/dot_general | solution.py:10
  166.3 31.7 %bitcast_dynamic-update-slice_fusion.6 = (bf16[4,512,1536]{2,1,0:T(8,128)(2,1)}, bf16[512,1536]{1,0:T(8,128)(2,1)}) fusion(bf16[4,512,1536]{2,1,0:T(8,128)(2,1)} %get-tuple-element.717, s32[]{:T(128)S(6)} %min.21, bf16[1,512,1536]{2,1,0:T(8,128)(2,1)S(1)} %constant_dynamic-slice_fusion.6, pred[]{:T(512)S(6)} %and.42, ...), kind=kOutput, calls=%fused_computation.15.clone.1 | convolution fusion | flops 19360382976 | bytes 48761344 | tf_op jit(solution)/shard_map/while/body/eval_jaxpr/dot_general | solution.py:10
  221.2 31.7 %bitcast_dynamic-update-slice_fusion.6 = (bf16[4,512,1536]{2,1,0:T(8,128)(2,1)}, bf16[512,1536]{1,0:T(8,128)(2,1)}) fusion(bf16[4,512,1536]{2,1,0:T(8,128)(2,1)} %get-tuple-element.717, s32[]{:T(128)S(6)} %min.21, bf16[1,512,1536]{2,1,0:T(8,128)(2,1)S(1)} %constant_dynamic-slice_fusion.6, pred[]{:T(512)S(6)} %and.42, ...), kind=kOutput, calls=%fused_computation.15.clone.1 | convolution fusion | flops 19360382976 | bytes 48761344 | tf_op jit(solution)/shard_map/while/body/eval_jaxpr/dot_general | solution.py:10
  276.4 31.7 %bitcast_dynamic-update-slice_fusion.6 = (bf16[4,512,1536]{2,1,0:T(8,128)(2,1)}, bf16[512,1536]{1,0:T(8,128)(2,1)}) fusion(bf16[4,512,1536]{2,1,0:T(8,128)(2,1)} %get-tuple-element.717, s32[]{:T(128)S(6)} %min.21, bf16[1,512,1536]{2,1,0:T(8,128)(2,1)S(1)} %constant_dynamic-slice_fusion.6, pred[]{:T(512)S(6)} %and.42, ...), kind=kOutput, calls=%fused_computation.15.clone.1 | convolution fusion | flops 19360382976 | bytes 48761344 | tf_op jit(solution)/shard_map/while/body/eval_jaxpr/dot_general | solution.py:10
  331.5 31.7 %bitcast_dynamic-update-slice_fusion.6 = (bf16[4,512,1536]{2,1,0:T(8,128)(2,1)}, bf16[512,1536]{1,0:T(8,128)(2,1)}) fusion(bf16[4,512,1536]{2,1,0:T(8,128)(2,1)} %get-tuple-element.717, s32[]{:T(128)S(6)} %min.21, bf16[1,512,1536]{2,1,0:T(8,128)(2,1)S(1)} %constant_dynamic-slice_fusion.6, pred[]{:T(512)S(6)} %and.42, ...), kind=kOutput, calls=%fused_computation.15.clone.1 | convolution fusion | flops 19360382976 | bytes 48761344 | tf_op jit(solution)/shard_map/while/body/eval_jaxpr/dot_general | solution.py:10
  388.3 866.0 %while.40 = (s32[]{:T(128)}, bf16[512,1536]{1,0:T(8,128)(2,1)S(1)}, bf16[4,512,1536]{2,1,0:T(8,128)(2,1)}, f32[1536,6144]{1,0:T(8,128)}, f32[6144,1536]{1,0:T(8,...) while((s32[]{:T(128)}, bf16[512,1536]{1,0:T(8,128)(2,1)S(1)}, ...), condition=%wide.region_4.5_spmd.clone, body=%wide.region_3.4_spmd.clone.sunk | while | flops 48470163456 | bytes 297271584 | solution.py:81
  409.6 21.7 %fusion.90 = bf16[512,6144]{1,0:T(8,128)(2,1)} fusion(f32[512,6144]{1,0:T(8,128)} %fusion.89, bf16[512,1536]{1,0:T(8,128)(2,1)S(1)} %bitcast_select_fusion.12, bf16[1,6144,1536]{2,1,0:T(8,128)(2,1)} %get-tuple-element.782), kind=kOutput, calls=%fused_computation.43.clone.1 | convolution fusion | flops 9726590976 | bytes 39321600 | tf_op jit(solution)/shard_map/while/body/eval_jaxpr/dot_general | solution.py:16
  511.3 21.7 %fusion.90 = bf16[512,6144]{1,0:T(8,128)(2,1)} fusion(f32[512,6144]{1,0:T(8,128)} %fusion.89, bf16[512,1536]{1,0:T(8,128)(2,1)S(1)} %bitcast_select_fusion.12, bf16[1,6144,1536]{2,1,0:T(8,128)(2,1)} %get-tuple-element.782), kind=kOutput, calls=%fused_computation.43.clone.1 | convolution fusion | flops 9726590976 | bytes 39321600 | tf_op jit(solution)/shard_map/while/body/eval_jaxpr/dot_general | solution.py:16
  551.3 34.3 %select_add_fusion.5 = f32[6144,1536]{1,0:T(8,128)} fusion(f32[6144,1536]{1,0:T(8,128)} %get-tuple-element.762, bf16[512,1536]{1,0:T(8,128)(2,1)S(1)} %bitcast_select_fusion.12, pred[]{:T(512)S(6)} %compare.3, pred[]{:T(512)S(6)} %and.43, f32[512,6144]{1,0:T(8,128)} %fusion.89), kind=kOutput, calls=%fused_computation.27.clone.1 | convolution fusion | flops 9720299520 | bytes 89653248 | tf_op jit(solution)/shard_map/while/body/eval_jaxpr/dot_general | solution.py:18
  585.5 31.9 %select_add_fusion.4 = f32[1536,6144]{1,0:T(8,128)} fusion(f32[1536,6144]{1,0:T(8,128)} %get-tuple-element.761, bf16[512,6144]{1,0:T(8,128)(2,1)} %fusion.90, pred[]{:T(512)S(6)} %compare.3, pred[]{:T(512)S(6)} %and.43, bf16[4,1,512,1536]{3,2,1,0:T(8,128)(2,1)} %get-tuple-element.783, s32[]{:T(128)S(6)} %min.22), kind=kOutput, calls=%fused_computation.28.clone.1 | convolution fusion | flops 9691987968 | bytes 83361800 | tf_op jit(solution)/shard_map/while/body/eval_jaxpr/dot_general | solution.py:19
  678.7 34.3 %select_add_fusion.5 = f32[6144,1536]{1,0:T(8,128)} fusion(f32[6144,1536]{1,0:T(8,128)} %get-tuple-element.762, bf16[512,1536]{1,0:T(8,128)(2,1)S(1)} %bitcast_select_fusion.12, pred[]{:T(512)S(6)} %compare.3, pred[]{:T(512)S(6)} %and.43, f32[512,6144]{1,0:T(8,128)} %fusion.89), kind=kOutput, calls=%fused_computation.27.clone.1 | convolution fusion | flops 9720299520 | bytes 89653248 | tf_op jit(solution)/shard_map/while/body/eval_jaxpr/dot_general | solution.py:18
  712.9 31.9 %select_add_fusion.4 = f32[1536,6144]{1,0:T(8,128)} fusion(f32[1536,6144]{1,0:T(8,128)} %get-tuple-element.761, bf16[512,6144]{1,0:T(8,128)(2,1)} %fusion.90, pred[]{:T(512)S(6)} %compare.3, pred[]{:T(512)S(6)} %and.43, bf16[4,1,512,1536]{3,2,1,0:T(8,128)(2,1)} %get-tuple-element.783, s32[]{:T(128)S(6)} %min.22), kind=kOutput, calls=%fused_computation.28.clone.1 | convolution fusion | flops 9691987968 | bytes 83361800 | tf_op jit(solution)/shard_map/while/body/eval_jaxpr/dot_general | solution.py:19
  806.1 34.3 %select_add_fusion.5 = f32[6144,1536]{1,0:T(8,128)} fusion(f32[6144,1536]{1,0:T(8,128)} %get-tuple-element.762, bf16[512,1536]{1,0:T(8,128)(2,1)S(1)} %bitcast_select_fusion.12, pred[]{:T(512)S(6)} %compare.3, pred[]{:T(512)S(6)} %and.43, f32[512,6144]{1,0:T(8,128)} %fusion.89), kind=kOutput, calls=%fused_computation.27.clone.1 | convolution fusion | flops 9720299520 | bytes 89653248 | tf_op jit(solution)/shard_map/while/body/eval_jaxpr/dot_general | solution.py:18
  840.3 31.9 %select_add_fusion.4 = f32[1536,6144]{1,0:T(8,128)} fusion(f32[1536,6144]{1,0:T(8,128)} %get-tuple-element.761, bf16[512,6144]{1,0:T(8,128)(2,1)} %fusion.90, pred[]{:T(512)S(6)} %compare.3, pred[]{:T(512)S(6)} %and.43, bf16[4,1,512,1536]{3,2,1,0:T(8,128)(2,1)} %get-tuple-element.783, s32[]{:T(128)S(6)} %min.22), kind=kOutput, calls=%fused_computation.28.clone.1 | convolution fusion | flops 9691987968 | bytes 83361800 | tf_op jit(solution)/shard_map/while/body/eval_jaxpr/dot_general | solution.py:19
  933.5 34.3 %select_add_fusion.5 = f32[6144,1536]{1,0:T(8,128)} fusion(f32[6144,1536]{1,0:T(8,128)} %get-tuple-element.762, bf16[512,1536]{1,0:T(8,128)(2,1)S(1)} %bitcast_select_fusion.12, pred[]{:T(512)S(6)} %compare.3, pred[]{:T(512)S(6)} %and.43, f32[512,6144]{1,0:T(8,128)} %fusion.89), kind=kOutput, calls=%fused_computation.27.clone.1 | convolution fusion | flops 9720299520 | bytes 89653248 | tf_op jit(solution)/shard_map/while/body/eval_jaxpr/dot_general | solution.py:18
  967.8 31.8 %select_add_fusion.4 = f32[1536,6144]{1,0:T(8,128)} fusion(f32[1536,6144]{1,0:T(8,128)} %get-tuple-element.761, bf16[512,6144]{1,0:T(8,128)(2,1)} %fusion.90, pred[]{:T(512)S(6)} %compare.3, pred[]{:T(512)S(6)} %and.43, bf16[4,1,512,1536]{3,2,1,0:T(8,128)(2,1)} %get-tuple-element.783, s32[]{:T(128)S(6)} %min.22), kind=kOutput, calls=%fused_computation.28.clone.1 | convolution fusion | flops 9691987968 | bytes 83361800 | tf_op jit(solution)/shard_map/while/body/eval_jaxpr/dot_general | solution.py:19
  1061.0 33.9 %select_add_fusion.5 = f32[6144,1536]{1,0:T(8,128)} fusion(f32[6144,1536]{1,0:T(8,128)} %get-tuple-element.762, bf16[512,1536]{1,0:T(8,128)(2,1)S(1)} %bitcast_select_fusion.12, pred[]{:T(512)S(6)} %compare.3, pred[]{:T(512)S(6)} %and.43, f32[512,6144]{1,0:T(8,128)} %fusion.89), kind=kOutput, calls=%fused_computation.27.clone.1 | convolution fusion | flops 9720299520 | bytes 89653248 | tf_op jit(solution)/shard_map/while/body/eval_jaxpr/dot_general | solution.py:18
  1094.9 32.0 %select_add_fusion.4 = f32[1536,6144]{1,0:T(8,128)} fusion(f32[1536,6144]{1,0:T(8,128)} %get-tuple-element.761, bf16[512,6144]{1,0:T(8,128)(2,1)} %fusion.90, pred[]{:T(512)S(6)} %compare.3, pred[]{:T(512)S(6)} %and.43, bf16[4,1,512,1536]{3,2,1,0:T(8,128)(2,1)} %get-tuple-element.783, s32[]{:T(128)S(6)} %min.22), kind=kOutput, calls=%fused_computation.28.clone.1 | convolution fusion | flops 9691987968 | bytes 83361800 | tf_op jit(solution)/shard_map/while/body/eval_jaxpr/dot_general | solution.py:19
  1188.1 34.3 %select_add_fusion.5 = f32[6144,1536]{1,0:T(8,128)} fusion(f32[6144,1536]{1,0:T(8,128)} %get-tuple-element.762, bf16[512,1536]{1,0:T(8,128)(2,1)S(1)} %bitcast_select_fusion.12, pred[]{:T(512)S(6)} %compare.3, pred[]{:T(512)S(6)} %and.43, f32[512,6144]{1,0:T(8,128)} %fusion.89), kind=kOutput, calls=%fused_computation.27.clone.1 | convolution fusion | flops 9720299520 | bytes 89653248 | tf_op jit(solution)/shard_map/while/body/eval_jaxpr/dot_general | solution.py:18
  1222.4 31.9 %select_add_fusion.4 = f32[1536,6144]{1,0:T(8,128)} fusion(f32[1536,6144]{1,0:T(8,128)} %get-tuple-element.761, bf16[512,6144]{1,0:T(8,128)(2,1)} %fusion.90, pred[]{:T(512)S(6)} %compare.3, pred[]{:T(512)S(6)} %and.43, bf16[4,1,512,1536]{3,2,1,0:T(8,128)(2,1)} %get-tuple-element.783, s32[]{:T(128)S(6)} %min.22), kind=kOutput, calls=%fused_computation.28.clone.1 | convolution fusion | flops 9691987968 | bytes 83361800 | tf_op jit(solution)/shard_map/while/body/eval_jaxpr/dot_general | solution.py:19
  1254.3 238.9 %all-reduce.3.cloned.1.call-done = (bf16[4,512,1536]{2,1,0:T(8,128)(2,1)}, bf16[4,512,1536]{2,1,0:T(8,128)(2,1)}) async-done(((bf16[4,512,1536]{2,1,0:T(8,128)(2,1)}, bf16[4,512,1536]{2,1,0:T(8,128)(2,1)}), (bf16[4,512,1536]{2,1,0:T(8,128)(2,1)}, bf16[4,512,1536]{2,1,0:T(8,128)(2,1)})) %all-reduce.3.cloned.1.call-update) | async-done | bytes 12582928 | tf_op jit(solution)/shard_map/psum | solution.py:82
  (118 shorter events, 593.3 us)
Async XLA Ops:
  7.2 1486.0 %all-reduce.3.cloned.1.call-start = ((), (), s32[]{:S(2)}) async-start(), calls=%async_computation | async-start | bytes 25165824 | tf_op jit(solution)/shard_map/psum | solution.py:82
  46.9 7.4 collective-permute-start
  87.8 21.7 %collective-permute-start = (bf16[512,1536]{1,0:T(8,128)(2,1)}, bf16[512,1536]{1,0:T(8,128)(2,1)S(1)}, u32[]{:S(2)}, u32[]{:S(2)}) collective-permute-start(bf16[512,1536]{1,0:T(8,128)(2,1)} %get-tuple-element.684), channel_id=1, source_target_pairs={{0,1},{1,2},{2,3},{4,5},{5,6},{6,7},{8,9},{9,10},{10,11},{12,13},{... | collective-permute-start | bytes 4718600 | tf_op jit(solution)/shard_map/while/body/eval_jaxpr/ppermute | solution.py:55
  142.8 21.8 %collective-permute-start = (bf16[512,1536]{1,0:T(8,128)(2,1)}, bf16[512,1536]{1,0:T(8,128)(2,1)S(1)}, u32[]{:S(2)}, u32[]{:S(2)}) collective-permute-start(bf16[512,1536]{1,0:T(8,128)(2,1)} %get-tuple-element.684), channel_id=1, source_target_pairs={{0,1},{1,2},{2,3},{4,5},{5,6},{6,7},{8,9},{9,10},{10,11},{12,13},{... | collective-permute-start | bytes 4718600 | tf_op jit(solution)/shard_map/while/body/eval_jaxpr/ppermute | solution.py:55
  198.0 21.5 %collective-permute-start = (bf16[512,1536]{1,0:T(8,128)(2,1)}, bf16[512,1536]{1,0:T(8,128)(2,1)S(1)}, u32[]{:S(2)}, u32[]{:S(2)}) collective-permute-start(bf16[512,1536]{1,0:T(8,128)(2,1)} %get-tuple-element.684), channel_id=1, source_target_pairs={{0,1},{1,2},{2,3},{4,5},{5,6},{6,7},{8,9},{9,10},{10,11},{12,13},{... | collective-permute-start | bytes 4718600 | tf_op jit(solution)/shard_map/while/body/eval_jaxpr/ppermute | solution.py:55
  252.9 21.8 %collective-permute-start = (bf16[512,1536]{1,0:T(8,128)(2,1)}, bf16[512,1536]{1,0:T(8,128)(2,1)S(1)}, u32[]{:S(2)}, u32[]{:S(2)}) collective-permute-start(bf16[512,1536]{1,0:T(8,128)(2,1)} %get-tuple-element.684), channel_id=1, source_target_pairs={{0,1},{1,2},{2,3},{4,5},{5,6},{6,7},{8,9},{9,10},{10,11},{12,13},{... | collective-permute-start | bytes 4718600 | tf_op jit(solution)/shard_map/while/body/eval_jaxpr/ppermute | solution.py:55
  308.2 21.7 %collective-permute-start = (bf16[512,1536]{1,0:T(8,128)(2,1)}, bf16[512,1536]{1,0:T(8,128)(2,1)S(1)}, u32[]{:S(2)}, u32[]{:S(2)}) collective-permute-start(bf16[512,1536]{1,0:T(8,128)(2,1)} %get-tuple-element.684), channel_id=1, source_target_pairs={{0,1},{1,2},{2,3},{4,5},{5,6},{6,7},{8,9},{9,10},{10,11},{12,13},{... | collective-permute-start | bytes 4718600 | tf_op jit(solution)/shard_map/while/body/eval_jaxpr/ppermute | solution.py:55
  363.2 21.7 %collective-permute-start = (bf16[512,1536]{1,0:T(8,128)(2,1)}, bf16[512,1536]{1,0:T(8,128)(2,1)S(1)}, u32[]{:S(2)}, u32[]{:S(2)}) collective-permute-start(bf16[512,1536]{1,0:T(8,128)(2,1)} %get-tuple-element.684), channel_id=1, source_target_pairs={{0,1},{1,2},{2,3},{4,5},{5,6},{6,7},{8,9},{9,10},{10,11},{12,13},{... | collective-permute-start | bytes 4718600 | tf_op jit(solution)/shard_map/while/body/eval_jaxpr/ppermute | solution.py:55
  409.6 21.7 %copy-start = (bf16[1,512,1536]{2,1,0:T(8,128)(2,1)S(1)}, bf16[1,512,1536]{2,1,0:T(8,128)(2,1)}, u32[]{:S(2)}) copy-start(bf16[1,512,1536]{2,1,0:T(8,128)(2,1)} %constant_dynamic-slice_fusion.8) | copy-start | bytes 4718596 | tf_op jit(solution)/shard_map/while
  448.3 41.7 %collective-permute-start.1 = (bf16[512,1536]{1,0:T(8,128)(2,1)}, bf16[512,1536]{1,0:T(8,128)(2,1)S(1)}, u32[]{:S(2)}, u32[]{:S(2)}) collective-permute-start(bf16[512,1536]{1,0:T(8,128)(2,1)} %get-tuple-element.698), channel_id=1, source_target_pairs={{1,0},{2,1},{3,2},{5,4},{6,5},{7,6},{9,8},{10,9},{11,10},{13,12},{... | collective-permute-start | bytes 4718600 | tf_op jit(solution)/shard_map/while/body/eval_jaxpr/ppermute | solution.py:76
  511.3 21.7 %copy-start = (bf16[1,512,1536]{2,1,0:T(8,128)(2,1)S(1)}, bf16[1,512,1536]{2,1,0:T(8,128)(2,1)}, u32[]{:S(2)}) copy-start(bf16[1,512,1536]{2,1,0:T(8,128)(2,1)} %constant_dynamic-slice_fusion.8) | copy-start | bytes 4718596 | tf_op jit(solution)/shard_map/while
  550.0 67.4 %collective-permute-start.1 = (bf16[512,1536]{1,0:T(8,128)(2,1)}, bf16[512,1536]{1,0:T(8,128)(2,1)S(1)}, u32[]{:S(2)}, u32[]{:S(2)}) collective-permute-start(bf16[512,1536]{1,0:T(8,128)(2,1)} %get-tuple-element.698), channel_id=1, source_target_pairs={{1,0},{2,1},{3,2},{5,4},{6,5},{7,6},{9,8},{10,9},{11,10},{13,12},{... | collective-permute-start | bytes 4718600 | tf_op jit(solution)/shard_map/while/body/eval_jaxpr/ppermute | solution.py:76
  638.7 21.7 %copy-start = (bf16[1,512,1536]{2,1,0:T(8,128)(2,1)S(1)}, bf16[1,512,1536]{2,1,0:T(8,128)(2,1)}, u32[]{:S(2)}) copy-start(bf16[1,512,1536]{2,1,0:T(8,128)(2,1)} %constant_dynamic-slice_fusion.8) | copy-start | bytes 4718596 | tf_op jit(solution)/shard_map/while
  677.4 67.4 %collective-permute-start.1 = (bf16[512,1536]{1,0:T(8,128)(2,1)}, bf16[512,1536]{1,0:T(8,128)(2,1)S(1)}, u32[]{:S(2)}, u32[]{:S(2)}) collective-permute-start(bf16[512,1536]{1,0:T(8,128)(2,1)} %get-tuple-element.698), channel_id=1, source_target_pairs={{1,0},{2,1},{3,2},{5,4},{6,5},{7,6},{9,8},{10,9},{11,10},{13,12},{... | collective-permute-start | bytes 4718600 | tf_op jit(solution)/shard_map/while/body/eval_jaxpr/ppermute | solution.py:76
  766.1 21.7 %copy-start = (bf16[1,512,1536]{2,1,0:T(8,128)(2,1)S(1)}, bf16[1,512,1536]{2,1,0:T(8,128)(2,1)}, u32[]{:S(2)}) copy-start(bf16[1,512,1536]{2,1,0:T(8,128)(2,1)} %constant_dynamic-slice_fusion.8) | copy-start | bytes 4718596 | tf_op jit(solution)/shard_map/while
  804.8 67.4 %collective-permute-start.1 = (bf16[512,1536]{1,0:T(8,128)(2,1)}, bf16[512,1536]{1,0:T(8,128)(2,1)S(1)}, u32[]{:S(2)}, u32[]{:S(2)}) collective-permute-start(bf16[512,1536]{1,0:T(8,128)(2,1)} %get-tuple-element.698), channel_id=1, source_target_pairs={{1,0},{2,1},{3,2},{5,4},{6,5},{7,6},{9,8},{10,9},{11,10},{13,12},{... | collective-permute-start | bytes 4718600 | tf_op jit(solution)/shard_map/while/body/eval_jaxpr/ppermute | solution.py:76
  893.5 21.7 %copy-start = (bf16[1,512,1536]{2,1,0:T(8,128)(2,1)S(1)}, bf16[1,512,1536]{2,1,0:T(8,128)(2,1)}, u32[]{:S(2)}) copy-start(bf16[1,512,1536]{2,1,0:T(8,128)(2,1)} %constant_dynamic-slice_fusion.8) | copy-start | bytes 4718596 | tf_op jit(solution)/shard_map/while
  932.2 67.4 %collective-permute-start.1 = (bf16[512,1536]{1,0:T(8,128)(2,1)}, bf16[512,1536]{1,0:T(8,128)(2,1)S(1)}, u32[]{:S(2)}, u32[]{:S(2)}) collective-permute-start(bf16[512,1536]{1,0:T(8,128)(2,1)} %get-tuple-element.698), channel_id=1, source_target_pairs={{1,0},{2,1},{3,2},{5,4},{6,5},{7,6},{9,8},{10,9},{11,10},{13,12},{... | collective-permute-start | bytes 4718600 | tf_op jit(solution)/shard_map/while/body/eval_jaxpr/ppermute | solution.py:76
  1020.9 21.7 %copy-start = (bf16[1,512,1536]{2,1,0:T(8,128)(2,1)S(1)}, bf16[1,512,1536]{2,1,0:T(8,128)(2,1)}, u32[]{:S(2)}) copy-start(bf16[1,512,1536]{2,1,0:T(8,128)(2,1)} %constant_dynamic-slice_fusion.8) | copy-start | bytes 4718596 | tf_op jit(solution)/shard_map/while
  1059.7 67.2 %collective-permute-start.1 = (bf16[512,1536]{1,0:T(8,128)(2,1)}, bf16[512,1536]{1,0:T(8,128)(2,1)S(1)}, u32[]{:S(2)}, u32[]{:S(2)}) collective-permute-start(bf16[512,1536]{1,0:T(8,128)(2,1)} %get-tuple-element.698), channel_id=1, source_target_pairs={{1,0},{2,1},{3,2},{5,4},{6,5},{7,6},{9,8},{10,9},{11,10},{13,12},{... | collective-permute-start | bytes 4718600 | tf_op jit(solution)/shard_map/while/body/eval_jaxpr/ppermute | solution.py:76
  1148.1 21.7 %copy-start = (bf16[1,512,1536]{2,1,0:T(8,128)(2,1)S(1)}, bf16[1,512,1536]{2,1,0:T(8,128)(2,1)}, u32[]{:S(2)}) copy-start(bf16[1,512,1536]{2,1,0:T(8,128)(2,1)} %constant_dynamic-slice_fusion.8) | copy-start | bytes 4718596 | tf_op jit(solution)/shard_map/while
  1186.8 67.4 %collective-permute-start.1 = (bf16[512,1536]{1,0:T(8,128)(2,1)}, bf16[512,1536]{1,0:T(8,128)(2,1)S(1)}, u32[]{:S(2)}, u32[]{:S(2)}) collective-permute-start(bf16[512,1536]{1,0:T(8,128)(2,1)} %get-tuple-element.698), channel_id=1, source_target_pairs={{1,0},{2,1},{3,2},{5,4},{6,5},{7,6},{9,8},{10,9},{11,10},{13,12},{... | collective-permute-start | bytes 4718600 | tf_op jit(solution)/shard_map/while/body/eval_jaxpr/ppermute | solution.py:76
  1493.1 6.1 copy-start.1
Sparse Core Ops, SparseCore 0:
  1254.4 238.6 all-reduce.2
where the time goes:
time: 1510 us
  matrix products  1050 us (70%)
  waiting for transfers between devices  239 us (16%)
  starting transfers between devices  114 us (8%)
  local copies, waits for them, and re-layouts  59.3 us (4%)
  other arithmetic  33.1 us (2%)
    psum x1, waiting for transfers between devices, body(): y = lax.psum(y, 'stage')  239 us
    dot_general x7, matrix products, _bwd_layer(): jnp.dot(u.astype(jnp.bfloat16).T, g, preferred_element_type=jnp.float32)  227 us
    dot_general x7, matrix products, _fwd_layer(): jnp.dot(u, w2, preferred_element_type=jnp.float32)  222 us
    dot_general x7, matrix products, _bwd_layer(): dw1 = jnp.dot(h.T, dz, preferred_element_type=jnp.float32)  210 us
    dot_general x7, matrix products, _bwd_layer(): du = jnp.dot(g, w2.T, preferred_element_type=jnp.float32)  152 us
    dot_general x7, matrix products, _bwd_layer(): z = jnp.dot(h, w1, preferred_element_type=jnp.float32)  119 us
    dot_general x7, matrix products, _bwd_layer(): jnp.dot(dz, w1.T, preferred_element_type=jnp.float32)  119 us
    ppermute x7, starting transfers between devices, fwd_tick(): recv = lax.ppermute(h, 'stage', fwd_perm)  105 us
  transfers between devices with their start and end apart: 15, of which 1 were waited for; matrix products, arithmetic and copies ran while one was open for 31% of the time, Pallas kernels for 0%

commit v1 on v0

v1 whole, which is shorter than its diff:
```python
import functools

import jax
import jax.numpy as jnp
from jax import lax
from jax.experimental import pallas as pl
from jax.experimental.pallas import tpu as pltpu
from jax.sharding import PartitionSpec as P

MESH = pl.DeviceIdType.MESH
BF = jnp.bfloat16
F32 = jnp.float32
C0 = 0.7978845608028654
C1 = C0 * 0.044715


def _gelu(z):
    t = jnp.tanh(z * (C0 + C1 * (z * z)))
    h = 0.5 * z
    return h + h * t


def _dgelu(z):
    z2 = z * z
    t = jnp.tanh(z * (C0 + C1 * z2))
    return 0.5 * (1.0 + t) + (0.5 * z) * (1.0 - t * t) * (C0 + (3.0 * C1) * z2)


def _dot(a, b):
    return jnp.dot(a, b, preferred_element_type=F32)


def _dot_t(a, b):
    return lax.dot_general(a, b, (((1,), (1,)), ((), ())), preferred_element_type=F32)


def _pass_kernel(C, T, S, NT, x_hbm, g_hbm, w1_hbm, w2_hbm,
                 y, dx, hs, gs, us, dzs, zb,
                 w1, w2, h, g, ub, zs, obf, obb,
                 wsem, hsem, gsem, ysem, dxsem, fsem, bsem, ysend, dsend, hss, gss, zsem, usem):
    n_tok, D = h.shape
    F = w1.shape[1]
    nch, nt, nn = n_tok // C, F // T, D // NT
    s = lax.axis_index("stage")
    first, last = s == 0, s == 3

    def rows(c):
        return pl.ds(pl.multiple_of(c * C, C), C)

    def cols(n):
        return pl.ds(n * NT, NT)

    def local(src, dst, sem):
        return pltpu.make_async_copy(src, dst, sem)

    def got(ref, c, n, sem):
        v = ref.at[rows(c), cols(n)]
        return local(v, v, sem.at[c, n])

    def remote(src, dst, ssem, rsem, to):
        return pltpu.make_async_remote_copy(src, dst, ssem, rsem, device_id={"stage": to}, device_id_type=MESH)

    cw1 = local(w1_hbm, w1, wsem.at[0])
    cw2 = local(w2_hbm, w2, wsem.at[1])

    @pl.when(first)
    def _():
        for n in range(nn):
            local(x_hbm.at[rows(0), cols(n)], h.at[rows(0), cols(n)], hsem.at[0, n]).start()
    cw1.start()
    cw2.start()

    @pl.when(first)
    def _():
        for c in range(1, nch):
            for n in range(nn):
                local(x_hbm.at[rows(c), cols(n)], h.at[rows(c), cols(n)], hsem.at[c, n]).start()

    @pl.when(last)
    def _():
        for c in range(nch):
            for n in range(nn):
                local(g_hbm.at[rows(c), cols(n)], g.at[rows(c), cols(n)], gsem.at[c, n]).start()

    barrier = pltpu.get_barrier_semaphore()
    for d in range(1, 4):
        pl.semaphore_signal(barrier, inc=1, device_id={"stage": lax.rem(s + d, 4)}, device_id_type=MESH)
    pl.semaphore_wait(barrier, 3)
    cw1.wait()
    cw2.wait()

    def f_next(c, n):
        return remote(obf.at[c % 2, :, cols(n)], h.at[rows(c), cols(n)], fsem.at[c % 2, n], hsem.at[c, n], s + 1)

    def b_next(c, n):
        return remote(obb.at[c % 2, :, cols(n)], g.at[rows(c), cols(n)], bsem.at[c % 2, n], gsem.at[c, n], s - 1)

    def y_copies(c, n):
        src, dst = obf.at[c % 2, :, cols(n)], y.at[rows(c), cols(n)]
        return [remote(src, dst, ysend.at[1, c % 2, n], ysem.at[c, n], 1),
                remote(src, dst, ysend.at[2, c % 2, n], ysem.at[c, n], 2),
                local(src, dst, ysend.at[0, c % 2, n])]

    def dx_copies(c, n):
        src, dst = obb.at[c % 2, :, cols(n)], dx.at[rows(c), cols(n)]
        return [remote(src, dst, dsend.at[1, c % 2, n], dxsem.at[c, n], 2),
                remote(src, dst, dsend.at[2, c % 2, n], dxsem.at[c, n], 1),
                local(src, dst, dsend.at[0, c % 2, n])]

    def wait_sent(copies):
        for cp in copies[:-1]:
            cp.wait_send()
        copies[-1].wait()

    def f_wait(c):
        for n in range(nn):
            @pl.when(last)
            def _(n=n):
                wait_sent(y_copies(c, n))

            @pl.when(jnp.logical_not(last))
            def _(n=n):
                f_next(c, n).wait_send()

    def b_wait(c):
        for n in range(nn):
            @pl.when(first)
            def _(n=n):
                wait_sent(dx_copies(c, n))

            @pl.when(jnp.logical_not(first))
            def _(n=n):
                b_next(c, n).wait_send()

    def y_fwd(c, n):
        v = y.at[rows(c), cols(n)]
        return remote(v, v, ysend.at[0, c % 2, n], ysem.at[c, n], 0)

    def dx_fwd(c, n):
        v = dx.at[rows(c), cols(n)]
        return remote(v, v, dsend.at[0, c % 2, n], dxsem.at[c, n], 3)

    def z_out(c, j, k):
        return local(zs.at[k], zb.at[c, j], zsem.at[k])

    def z_in(c, j, k):
        return local(zb.at[c, j], zs.at[k], zsem.at[k])

    def save(dst, c):
        return local(ub, dst.at[rows(c), :], usem)

    def keep(src, dst, c, sem):
        return local(src.at[rows(c), :], dst.at[rows(c), :], sem.at[c])

    def fwd(c):
        for n in range(nn):
            got(h, c, n, hsem).wait()
        keep(h, hs, c, hss).start()
        hc = h.at[rows(c), :]

        def st1(j, _):
            k = j % 2

            @pl.when(j >= 2)
            def _():
                z_out(c, j - 2, k).wait()
            for i in range(T // S):
                col = pl.ds(pl.multiple_of(j * T + i * S, S), S)
                z = _dot(hc[...], w1[:, col])
                zs[k, :, i * S:(i + 1) * S] = z
                ub[:, col] = _gelu(z).astype(BF)
            z_out(c, j, k).start()
            return 0
        lax.fori_loop(0, nt, st1, 0)
        save(us, c).start()

        @pl.when(c >= 2)
        def _():
            f_wait(c - 2)

        def st2(n, _):
            col = pl.ds(pl.multiple_of(n * NT, NT), NT)
            obf[c % 2, :, col] = (hc[:, col].astype(F32) + _dot(ub[...], w2[:, col])).astype(BF)

            @pl.when(last)
            def _():
                src, dst = obf.at[c % 2, :, col], y.at[rows(c), col]
                remote(src, dst, ysend.at[1, c % 2, n], ysem.at[c, n], 1).start()
                remote(src, dst, ysend.at[2, c % 2, n], ysem.at[c, n], 2).start()
                local(src, dst, ysend.at[0, c % 2, n]).start()

            @pl.when(jnp.logical_not(last))
            def _():
                remote(obf.at[c % 2, :, col], h.at[rows(c), col], fsem.at[c % 2, n], hsem.at[c, n], s + 1).start()
            return 0
        lax.fori_loop(0, nn, st2, 0)
        for j in range(max(0, nt - 2), nt):
            z_out(c, j, j % 2).wait()
        save(us, c).wait()

    def bwd(c):
        z_in(c, 0, 0).start()
        for n in range(nn):
            got(g, c, n, gsem).wait()
        keep(g, gs, c, gss).start()
        gc = g.at[rows(c), :]

        def st1(j, _):
            k = j % 2

            @pl.when(j + 1 < nt)
            def _():
                z_in(c, j + 1, 1 - k).start()
            z_in(c, j, k).wait()
            for i in range(T // S):
                col = pl.ds(pl.multiple_of(j * T + i * S, S), S)
                du = _dot_t(gc[...], w2[col, :])
                ub[:, col] = (_dgelu(zs[k, :, i * S:(i + 1) * S]) * du).astype(BF)
            return 0
        lax.fori_loop(0, nt, st1, 0)
        save(dzs, c).start()

        @pl.when(c >= 2)
        def _():
            b_wait(c - 2)

        def st2(n, _):
            col = pl.ds(pl.multiple_of(n * NT, NT), NT)
            obb[c % 2, :, col] = (gc[:, col].astype(F32) + _dot_t(ub[...], w1[col, :])).astype(BF)

            @pl.when(first)
            def _():
                src, dst = obb.at[c % 2, :, col], dx.at[rows(c), col]
                remote(src, dst, dsend.at[1, c % 2, n], dxsem.at[c, n], 2).start()
                remote(src, dst, dsend.at[2, c % 2, n], dxsem.at[c, n], 1).start()
                local(src, dst, dsend.at[0, c % 2, n]).start()

            @pl.when(jnp.logical_not(first))
            def _():
                remote(obb.at[c % 2, :, col], g.at[rows(c), col], bsem.at[c % 2, n], gsem.at[c, n], s - 1).start()
            return 0
        lax.fori_loop(0, nn, st2, 0)
        save(dzs, c).wait()

        @pl.when(s == 1)
        def _():
            @pl.when(c >= 2)
            def _():
                for n in range(nn):
                    y_fwd(c - 2, n).wait_send()
            for n in range(nn):
                got(y, c, n, ysem).wait()
                y_fwd(c, n).start()

        @pl.when((s == 2) & (c >= 3))
        def _():
            pass_dx(c - 3)

    def pass_dx(c):
        @pl.when(c >= 2)
        def _():
            for n in range(nn):
                dx_fwd(c - 2, n).wait_send()
        for n in range(nn):
            got(dx, c, n, dxsem).wait()
            dx_fwd(c, n).start()

    def step(t, _):
        is_f = jnp.where(last, t % 2 == 0, t < nch)
        c = jnp.where(last, t // 2, jnp.where(t < nch, t, t - nch))

        @pl.when(is_f)
        def _():
            fwd(c)

        @pl.when(jnp.logical_not(is_f))
        def _():
            bwd(c)
        return 0
    lax.fori_loop(0, 2 * nch, step, 0)

    @pl.when(s == 2)
    def _():
        def rest(c, _):
            pass_dx(c)
            return 0
        lax.fori_loop(nch - 3, nch, rest, 0)

    def drain(c, _):
        f_wait(c)
        b_wait(c)

        @pl.when(s == 1)
        def _():
            for n in range(nn):
                y_fwd(c, n).wait_send()

        @pl.when(s == 2)
        def _():
            for n in range(nn):
                dx_fwd(c, n).wait_send()
        return 0
    lax.fori_loop(nch - 2, nch, drain, 0)

    def arrivals(c, _):
        keep(h, hs, c, hss).wait()
        keep(g, gs, c, gss).wait()
        for n in range(nn):
            @pl.when((s == 0) | (s == 2))
            def _(n=n):
                got(y, c, n, ysem).wait()

            @pl.when((s == 1) | (s == 3))
            def _(n=n):
                got(dx, c, n, dxsem).wait()
        return 0
    lax.fori_loop(0, nch, arrivals, 0)


def _run_pass(x, g, w1, w2, C=256, T=1536, S=512, NT=512):
    n_tok, D = x.shape
    F = w1.shape[1]
    nch, nt, nn = n_tok // C, F // T, D // NT
    any_ = pl.BlockSpec(memory_space=pl.ANY)
    act = jax.ShapeDtypeStruct((n_tok, D), BF)
    hid = jax.ShapeDtypeStruct((n_tok, F), BF)
    dma = pltpu.SemaphoreType.DMA
    return pl.pallas_call(
        functools.partial(_pass_kernel, C, T, S, NT),
        out_shape=(act, act, act, act, hid, hid, jax.ShapeDtypeStruct((nch, nt, C, T), F32)),
        in_specs=[any_] * 4,
        out_specs=(any_,) * 7,
        scratch_shapes=[
            pltpu.VMEM((D, F), BF), pltpu.VMEM((F, D), BF),
            pltpu.VMEM((n_tok, D), BF), pltpu.VMEM((n_tok, D), BF),
            pltpu.VMEM((C, F), BF), pltpu.VMEM((2, C, T), F32),
            pltpu.VMEM((2, C, D), BF), pltpu.VMEM((2, C, D), BF),
            dma((2,)), dma((nch, nn)), dma((nch, nn)), dma((nch, nn)), dma((nch, nn)),
            dma((2, nn)), dma((2, nn)), dma((3, 2, nn)), dma((3, 2, nn)),
            dma((nch,)), dma((nch,)), dma((2,)), dma,
        ],
        compiler_params=pltpu.CompilerParams(collective_id=0, has_side_effects=True, vmem_limit_bytes=67043328),
        name="mlp_pass",
    )(x, g, w1, w2)


def _dot_k0(a, b):
    return lax.dot_general(a, b, (((0,), (0,)), ((), ())), preferred_element_type=F32)


def solution(mesh):
    def body(x, g, w1, w2):
        shape = x.shape
        D = shape[-1]
        y, dx, hs, gs, us, dzs, _ = _run_pass(x.reshape(-1, D), g.reshape(-1, D), w1[0], w2[0])
        dw1 = _dot_k0(hs, dzs)
        dw2 = _dot_k0(us, gs)
        return y.reshape(shape), dx.reshape(shape), dw1[None], dw2[None]

    return jax.shard_map(body, mesh=mesh,
                         in_specs=(P('data'), P('data'), P('stage'), P('stage')),
                         out_specs=(P('data'), P('data'), P(('data', 'stage')), P(('data', 'stage'))),
                         check_vma=False)
```

time: 1510 us -> 430 us (0.28)
  matrix products: 1050 us -> 93.3 us
  Pallas kernels: 0 us -> 327 us
  waiting for transfers between devices: 239 us -> 0 us
  starting transfers between devices: 114 us -> 0 us
  local copies, waits for them, and re-layouts: 59.3 us -> 5.43 us
  other arithmetic: 33.1 us -> 0.01 us
    dot_general x42 -> x2, matrix products: 1050 us -> 93.3 us  [_dot_k0(): lax.dot_general(a, b, (((0,), (0,)), ((), ())), preferred_element_type=F32)]
    pallas_call x0 -> x1, Pallas kernels: none -> 327 us  [_run_pass(): pl.pallas_call(functools.partial(_pass_kernel, C, T, S, NT), out_shape=(a...]
    psum x1 -> x0, waiting for transfers between devices: 239 us -> none  [body(): y = lax.psum(y, 'stage')]
    ppermute x14 -> x0, starting transfers between devices: 114 us -> none  [the longest x7 105 us: fwd_tick(): recv = lax.ppermute(h, 'stage', fwd_perm)]
    dynamic_slice x21 -> x0, local copies, waits for them, and re-layouts: 40.1 us -> none  [_put(): old = lax.dynamic_index_in_dim(buf, i, 0, keepdims=False)]
    dynamic_update_slice x7 -> x0, other arithmetic: 22.1 us -> none  [_put(): return lax.dynamic_update_index_in_dim(buf, jnp.where(ok, val, old), i, 0)]
  transfers between devices with their start and end apart: 15 -> 0, of which waited for: 1 -> 0; matrix products, arithmetic and copies ran while one was open for 31% -> 0% of each run, Pallas kernels for 0% -> 0%
where the time goes in v1:
time: 430 us; the launch traced here: 427 us
  Pallas kernels  327 us (76%)
  matrix products  93.3 us (22%)
  local copies, waits for them, and re-layouts  5.43 us (1%)
    pallas_call x1, Pallas kernels, _run_pass(): pl.pallas_call(functools.partial(_pass_kernel, C, T, S, NT), out_shape=(a...  327 us
    dot_general x2, matrix products, _dot_k0(): lax.dot_general(a, b, (((0,), (0,)), ((), ())), preferred_element_type=F32)  93.3 us

profile of v1, /device:TPU:0, one launch (start us, length us, event | category | flops | bytes accessed | tf_op | source)
XLA Modules:
  0.0 426.8 jit_solution(14151288239365801637)
XLA Ops:
  0.6 327.5 %mlp_pass.1 = (bf16[2048,1536]{1,0:T(8,128)(2,1)}, bf16[2048,1536]{1,0:T(8,128)(2,1)}, bf16[2048,1536]{1,0:T(8,128)(2,1)}, bf16[2048,1536]{1,0:T(8,128)(2,1)}, b...) custom-call(bf16[2048,1536]{1,0:T(8,128)(2,1)} %bitcast.16, ...), custom_call_target="tpu_custom_call" | custom-call | tf_op jit(solution)/shard_map/mlp_pass/pallas_call | solution.py:328
  328.1 0.0 copy-start
  328.1 0.0 slice-start.2
  328.1 0.0 slice-start
  328.1 47.4 %convolution_bitcast_fusion.1 = f32[1,1536,6144]{2,1,0:T(8,128)} fusion(bf16[2048,1536]{1,0:T(8,128)(2,1)} %get-tuple-element.12, bf16[2048,6144]{1,0:T(8,128)(2,1)} %get-tuple-element.13), kind=kOutput, calls=%fused_computation.1 | convolution fusion | flops 38654705664 | bytes 69206016 | tf_op jit(solution)/shard_map/dot_general | solution.py:348
  375.6 0.0 copy-done
  375.6 0.0 slice-start.3
  375.6 0.0 slice-start.1
  375.6 45.8 %convolution_bitcast_fusion = f32[1,6144,1536]{2,1,0:T(8,128)} fusion(bf16[2048,6144]{1,0:T(8,128)(2,1)} %get-tuple-element.14, bf16[2048,1536]{1,0:T(8,128)(2,1)S(1)} %copy-done), kind=kOutput, calls=%fused_computation | convolution fusion | flops 38654705664 | bytes 69206016 | tf_op jit(solution)/shard_map/dot_general | solution.py:348
  421.4 0.0 slice-done.2
  421.4 0.0 slice-done.3
  421.4 2.7 copy.10
  424.1 0.0 slice-done
  424.1 0.0 slice-done.1
  424.1 2.7 copy.11
  (2 shorter events, 0.0 us)
Async XLA Ops:
  328.1 47.5 %copy-start = (bf16[2048,1536]{1,0:T(8,128)(2,1)S(1)}, bf16[2048,1536]{1,0:T(8,128)(2,1)}, u32[]{:S(2)}) copy-start(bf16[2048,1536]{1,0:T(8,128)(2,1)} %get-tuple-element.15) | copy-start | bytes 18874372
  328.1 93.3 %slice-start.2 = ((s8[6291456]{0:T(1024)(128)(4,1)}), s8[4194304]{0:T(1024)(128)(4,1)S(1)}, s32[]{:S(2)}) async-start(s8[6291456]{0:T(1024)(128)(4,1)} %bitcast.21), calls=%async_computation.2 | async-start | bytes 8388608
  328.1 96.0 %slice-start = ((s8[6291456]{0:T(1024)(128)(4,1)}), s8[4194304]{0:T(1024)(128)(4,1)S(1)}, s32[]{:S(2)}) async-start(s8[6291456]{0:T(1024)(128)(4,1)} %bitcast.18), calls=%async_computation | async-start | bytes 8388608
  375.6 45.9 %slice-start.3 = ((s8[6291456]{0:T(1024)(128)(4,1)}), s8[2097152]{0:T(1024)(128)(4,1)S(1)}, s32[]{:S(2)}) async-start(s8[6291456]{0:T(1024)(128)(4,1)} %bitcast.21), calls=%async_computation.3 | async-start | bytes 4194304
  375.6 48.6 %slice-start.1 = ((s8[6291456]{0:T(1024)(128)(4,1)}), s8[2097152]{0:T(1024)(128)(4,1)S(1)}, s32[]{:S(2)}) async-start(s8[6291456]{0:T(1024)(128)(4,1)} %bitcast.18), calls=%async_computation.1 | async-start | bytes 4194304

commit v2 on v1

v2 whole, which is shorter than its diff:
```python
import functools

import jax
import jax.numpy as jnp
from jax import lax
from jax.experimental import pallas as pl
from jax.experimental.pallas import tpu as pltpu
from jax.sharding import PartitionSpec as P

MESH = pl.DeviceIdType.MESH
BF = jnp.bfloat16
F32 = jnp.float32
C0 = 0.7978845608028654
C1 = C0 * 0.044715


def _act(z):
    q = C1 * (z * z)
    p = q + C0
    s = 1.0 + jnp.tanh(z * p)
    h = 0.5 * z
    return h * s, s * (0.5 + h * (2.0 - s) * (p + 2.0 * q))


def _dot(a, b):
    return jnp.dot(a, b, preferred_element_type=F32)


def _dot_t(a, b):
    return lax.dot_general(a, b, (((1,), (1,)), ((), ())), preferred_element_type=F32)


def _pass_kernel(C, T, NT, x_hbm, g_hbm, w1_hbm, w2_hbm,
                 y, dx, hs, gs, us, dzs, gb,
                 w1, w2, hg, ub, za, zb, gp, obf, obb,
                 wsem, hsem, gsem, ysem, dxsem, fsem, bsem, ysend, dsend, hss, gss, gsem2, usem):
    n_tok, D = x_hbm.shape
    F = w1.shape[1]
    hf = n_tok // C // 2
    nch, npair, nn = n_tok // C, F // (2 * T), D // NT
    s = lax.axis_index("stage")
    first, last = s == 0, s == 3
    inner = jnp.logical_not(last)

    def rows(c):
        return pl.ds(pl.multiple_of(c * C, C), C)

    def grows(c):
        return rows(jnp.where(c < hf, nch + c, c - hf))

    def cols(n):
        return pl.ds(n * NT if isinstance(n, int) else pl.multiple_of(n * NT, NT), NT)

    def local(src, dst, sem):
        return pltpu.make_async_copy(src, dst, sem)

    def got(ref, r, c, n, sem):
        v = ref.at[r, cols(n)]
        return local(v, v, sem.at[c, n])

    def remote(src, dst, ssem, rsem, to):
        return pltpu.make_async_remote_copy(src, dst, ssem, rsem, device_id={"stage": to}, device_id_type=MESH)

    def g_load(c, n):
        return local(g_hbm.at[rows(c), cols(n)], hg.at[grows(c), cols(n)], gsem.at[c, n])

    def w1_load(j):
        col = pl.ds(pl.multiple_of(j * T, T), T)
        return local(w1_hbm.at[:, col], w1.at[:, col], wsem.at[j])

    w2_load = local(w2_hbm, w2, wsem.at[F // T])

    @pl.when(first)
    def _():
        for n in range(nn):
            local(x_hbm.at[rows(0), cols(n)], hg.at[rows(0), cols(n)], hsem.at[0, n]).start()
    for j in range(F // T):
        w1_load(j).start()
    w2_load.start()

    @pl.when(first)
    def _():
        for c in range(1, nch):
            for n in range(nn):
                local(x_hbm.at[rows(c), cols(n)], hg.at[rows(c), cols(n)], hsem.at[c, n]).start()

    @pl.when(last)
    def _():
        for c in range(hf):
            for n in range(nn):
                g_load(c, n).start()

    barrier = pltpu.get_barrier_semaphore()
    for d in range(1, 4):
        pl.semaphore_signal(barrier, inc=1, device_id={"stage": lax.rem(s + d, 4)}, device_id_type=MESH)
    pl.semaphore_wait(barrier, 3)

    def f_next(c, n):
        return remote(obf.at[:, cols(n)], hg.at[rows(c), cols(n)], fsem.at[c % 2, n], hsem.at[c, n], s + 1)

    def b_next(c, n):
        return remote(obb.at[:, cols(n)], hg.at[grows(c), cols(n)], bsem.at[c % 2, n], gsem.at[c, n], s - 1)

    def y_copies(c, n):
        src, dst = obf.at[:, cols(n)], y.at[rows(c), cols(n)]
        return [remote(src, dst, ysend.at[1, c % 2, n], ysem.at[c, n], 1),
                remote(src, dst, ysend.at[2, c % 2, n], ysem.at[c, n], 2),
                local(src, dst, ysend.at[0, c % 2, n])]

    def dx_copies(c, n):
        src, dst = obb.at[:, cols(n)], dx.at[rows(c), cols(n)]
        return [remote(src, dst, dsend.at[1, c % 2, n], dxsem.at[c, n], 2),
                remote(src, dst, dsend.at[2, c % 2, n], dxsem.at[c, n], 1),
                local(src, dst, dsend.at[0, c % 2, n])]

    def wait_sent(copies):
        for cp in copies[:-1]:
            cp.wait_send()
        copies[-1].wait()

    def f_wait(c):
        for n in range(nn):
            @pl.when(last)
            def _(n=n):
                wait_sent(y_copies(c, n))

            @pl.when(jnp.logical_not(last))
            def _(n=n):
                f_next(c, n).wait_send()

    def b_wait(c):
        for n in range(nn):
            @pl.when(first)
            def _(n=n):
                wait_sent(dx_copies(c, n))

            @pl.when(jnp.logical_not(first))
            def _(n=n):
                b_next(c, n).wait_send()

    def y_fwd(c, n):
        v = y.at[rows(c), cols(n)]
        return remote(v, v, ysend.at[0, c % 2, n], ysem.at[c, n], 0)

    def dx_fwd(c, n):
        v = dx.at[rows(c), cols(n)]
        return remote(v, v, dsend.at[0, c % 2, n], dxsem.at[c, n], 3)

    def gp_out(c, i):
        return local(gp.at[i], gb.at[c, i], gsem2.at[i])

    def gp_in(c, i):
        return local(gb.at[c, i], gp.at[i], gsem2.at[i])

    def save(dst, c):
        return local(ub, dst.at[rows(c), :], usem.at[0])

    def u_head(c):
        return local(ub.at[:, :F - 2 * T], us.at[rows(c), :F - 2 * T], usem.at[1])

    def u_tail(c):
        return local(ub.at[:, F - 2 * T:], us.at[rows(c), F - 2 * T:], usem.at[2])

    def keep(r, dst, c, sem):
        return local(hg.at[r, :], dst.at[rows(c), :], sem.at[c])

    def fwd(c):
        for n in range(nn):
            got(hg, rows(c), c, n, hsem).wait()
        keep(rows(c), hs, c, hss).start()
        hc = hg.at[rows(c), :]

        def act(zr, k, half, off):
            for r in range(0, C, 16):
                u, d = _act(zr[r:r + 16])
                ub[r:r + 16, pl.ds(off, T)] = u.astype(BF)
                gp[k, half, r:r + 16] = d

        def zdot(zr, off):
            for j in range(0, T, NT):
                zr[:, j:j + NT] = _dot(hc[...], w1[:, pl.ds(off + j, NT)])

        @pl.when(c == 0)
        def _():
            w1_load(0).wait()
        zdot(za, 0)

        def st1(i, _):
            @pl.when(inner & (c >= 1))
            def _():
                gp_out(c - 1, i).wait()

            @pl.when(c == 0)
            def _():
                w1_load(2 * i + 1).wait()
                w1_load(2 * i + 2).wait()
            o = pl.multiple_of(2 * i * T, 2 * T)
            act(za, i, 0, o)
            zdot(zb, o + T)
            act(zb, i, 1, o + T)
            zdot(za, o + 2 * T)

            @pl.when(inner)
            def _():
                gp_out(c, i).start()
            return 0
        lax.fori_loop(0, npair - 1, st1, 0)
        u_head(c).start()
        i = npair - 1
        o = 2 * i * T

        @pl.when(c >= 1)
        def _():
            f_wait(c - 1)

        @pl.when(inner & (c >= 1))
        def _():
            gp_out(c - 1, i).wait()
            u_tail(c - 1).wait()

        @pl.when(c == 0)
        def _():
            w1_load(F // T - 1).wait()
            w2_load.wait()
        act(za, i, 0, o)
        zdot(zb, o + T)
        def out(n, col, a):
            obf[:, col] = (hc[:, col].astype(F32) + a).astype(BF)

            @pl.when(last)
            def _():
                for cp in y_copies(c, n):
                    cp.start()

            @pl.when(inner)
            def _():
                f_next(c, n).start()

        keep(rows(c), hs, c, hss).wait()
        a = _dot(ub[:, :F - T], w2[:F - T, cols(0)])
        act(zb, i, 1, o + T)
        out(0, cols(0), a + _dot(ub[:, F - T:], w2[F - T:, cols(0)]))
        u_tail(c).start()

        def st2(n, _):
            out(n, cols(n), _dot(ub[...], w2[:, cols(n)]))
            return 0
        lax.fori_loop(1, nn, st2, 0)

        @pl.when(last & (c < hf))
        def _():
            for n in range(nn):
                g_load(c + hf, n).start()

        @pl.when(inner)
        def _():
            gp_out(c, i).start()
        u_head(c).wait()

    def bwd(c):
        @pl.when(inner & (c == 0))
        def _():
            for i in range(npair):
                gp_out(nch - 1, i).wait()
                gp_in(0, i).start()
        for n in range(nn):
            got(hg, grows(c), c, n, gsem).wait()
        keep(grows(c), gs, c, gss).start()
        gc = hg.at[grows(c), :]

        def st1(i, _):
            @pl.when(inner)
            def _():
                gp_in(c, i).wait()

            @pl.when((i == npair - 1) & (last | (c == 0)))
            def _():
                u_tail(jnp.where(last, c, nch - 1)).wait()
            for q in range(2):
                for j in range(0, T, NT):
                    col = pl.ds(pl.multiple_of((2 * i + q) * T + j, NT), NT)
                    ub[:, col] = (gp[i, q, :, j:j + NT] * _dot_t(gc[...], w2[col, :])).astype(BF)
            return 0
        lax.fori_loop(0, npair, st1, 0)
        save(dzs, c).start()

        @pl.when(inner & (c + 1 < nch))
        def _():
            for i in range(npair):
                gp_in(c + 1, i).start()

        @pl.when(c >= 1)
        def _():
            b_wait(c - 1)
        def st2(n, _):
            col = cols(n)
            obb[:, col] = (gc[:, col].astype(F32) + _dot_t(ub[...], w1[col, :])).astype(BF)

            @pl.when(first)
            def _():
                for cp in dx_copies(c, n):
                    cp.start()

            @pl.when(jnp.logical_not(first))
            def _():
                b_next(c, n).start()
            return 0
        lax.fori_loop(0, nn, st2, 0)
        save(dzs, c).wait()

        @pl.when(s == 1)
        def _():
            @pl.when(c >= 2)
            def _():
                for n in range(nn):
                    y_fwd(c - 2, n).wait_send()
            for n in range(nn):
                got(y, rows(c), c, n, ysem).wait()
                y_fwd(c, n).start()

        @pl.when((s == 2) & (c >= 3))
        def _():
            pass_dx(c - 3)

    def pass_dx(c):
        @pl.when(c >= 2)
        def _():
            for n in range(nn):
                dx_fwd(c - 2, n).wait_send()
        for n in range(nn):
            got(dx, rows(c), c, n, dxsem).wait()
            dx_fwd(c, n).start()

    def step(t, _):
        is_f = jnp.where(last, t % 2 == 0, t < nch)
        c = jnp.where(last, t // 2, jnp.where(t < nch, t, t - nch))

        @pl.when(is_f)
        def _():
            fwd(c)

        @pl.when(jnp.logical_not(is_f))
        def _():
            bwd(c)
        return 0
    lax.fori_loop(0, 2 * nch, step, 0)

    @pl.when(s == 2)
    def _():
        def rest(c, _):
            pass_dx(c)
            return 0
        lax.fori_loop(nch - 3, nch, rest, 0)

    f_wait(nch - 1)
    b_wait(nch - 1)

    def drain(c, _):

        @pl.when(s == 1)
        def _():
            for n in range(nn):
                y_fwd(c, n).wait_send()

        @pl.when(s == 2)
        def _():
            for n in range(nn):
                dx_fwd(c, n).wait_send()
        return 0
    lax.fori_loop(nch - 2, nch, drain, 0)

    def arrivals(c, _):
        keep(grows(c), gs, c, gss).wait()
        for n in range(nn):
            @pl.when((s == 0) | (s == 2))
            def _(n=n):
                got(y, rows(c), c, n, ysem).wait()

            @pl.when((s == 1) | (s == 3))
            def _(n=n):
                got(dx, rows(c), c, n, dxsem).wait()
        return 0
    lax.fori_loop(0, nch, arrivals, 0)


def _run_pass(x, g, w1, w2, C=256, T=1024, NT=512):
    n_tok, D = x.shape
    F = w1.shape[1]
    nch, npair, nn = n_tok // C, F // (2 * T), D // NT
    any_ = pl.BlockSpec(memory_space=pl.ANY)
    act = jax.ShapeDtypeStruct((n_tok, D), BF)
    hid = jax.ShapeDtypeStruct((n_tok, F), BF)
    dma = pltpu.SemaphoreType.DMA
    return pl.pallas_call(
        functools.partial(_pass_kernel, C, T, NT),
        out_shape=(act, act, act, act, hid, hid, jax.ShapeDtypeStruct((nch, npair, 2, C, T), F32)),
        in_specs=[any_] * 4,
        out_specs=(any_,) * 7,
        scratch_shapes=[
            pltpu.VMEM((D, F), BF), pltpu.VMEM((F, D), BF),
            pltpu.VMEM((n_tok + n_tok // 2, D), BF),
            pltpu.VMEM((C, F), BF), pltpu.VMEM((C, T), F32), pltpu.VMEM((C, T), F32),
            pltpu.VMEM((npair, 2, C, T), F32),
            pltpu.VMEM((C, D), BF), pltpu.VMEM((C, D), BF),
            dma((F // T + 1,)), dma((nch, nn)), dma((nch, nn)), dma((nch, nn)), dma((nch, nn)),
            dma((2, nn)), dma((2, nn)), dma((3, 2, nn)), dma((3, 2, nn)),
            dma((nch,)), dma((nch,)), dma((npair,)), dma((3,)),
        ],
        compiler_params=pltpu.CompilerParams(collective_id=0, has_side_effects=True, vmem_limit_bytes=67043328),
        name="mlp_pass",
    )(x, g, w1, w2)


def _dot_k0(a, b):
    return lax.dot_general(a, b, (((0,), (0,)), ((), ())), preferred_element_type=F32)


def _grad_kernel(n1, x_any, g_any, yi, dxi, dz, u, yo, dxo, dw1, dw2, h, g, sem):
    i = pl.program_id(0)
    ch = pltpu.make_async_copy(x_any, h, sem.at[0])
    cg = pltpu.make_async_copy(g_any, g, sem.at[1])

    @pl.when(i == 0)
    def _():
        ch.start()
        cg.start()
        ch.wait()
    yo[...] = yi[...]
    dxo[...] = dxi[...]

    @pl.when(i < n1)
    def _():
        dw1[...] = _dot_k0(h[...], dz[...])

    @pl.when(i == n1)
    def _():
        cg.wait()

    @pl.when(i >= n1)
    def _():
        dw2[...] = _dot_k0(u[...], g[...])


def _run_grads(hs, gs, us, dzs, y, dx, B=512):
    n_tok, D = hs.shape
    F = us.shape[1]
    n1 = F // B
    R = n_tok // 16
    any_ = pl.BlockSpec(memory_space=pl.ANY)
    act = pl.BlockSpec((R, D), lambda i: (jnp.minimum(i, 15), 0))
    one = lambda i: jnp.minimum(i, n1 - 1)
    two = lambda i: jnp.maximum(i - n1, 0)
    flops = 4 * n_tok * D * F
    return pl.pallas_call(
        functools.partial(_grad_kernel, n1),
        grid=(2 * n1,),
        in_specs=[any_, any_, act, act,
                  pl.BlockSpec((n_tok, B), lambda i: (0, one(i))), pl.BlockSpec((n_tok, B), lambda i: (0, two(i)))],
        out_specs=(act, act, pl.BlockSpec((D, B), lambda i: (0, one(i))), pl.BlockSpec((B, D), lambda i: (two(i), 0))),
        out_shape=(jax.ShapeDtypeStruct((n_tok, D), BF), jax.ShapeDtypeStruct((n_tok, D), BF),
                   jax.ShapeDtypeStruct((D, F), F32), jax.ShapeDtypeStruct((F, D), F32)),
        scratch_shapes=[pltpu.VMEM((n_tok, D), BF), pltpu.VMEM((n_tok, D), BF), pltpu.SemaphoreType.DMA((2,))],
        compiler_params=pltpu.CompilerParams(dimension_semantics=("arbitrary",), vmem_limit_bytes=67043328),
        cost_estimate=pl.CostEstimate(flops=flops, bytes_accessed=200 * 1024 * 1024, transcendentals=0),
        name="mlp_grads",
    )(hs, gs, y, dx, dzs, us)


def solution(mesh):
    def body(x, g, w1, w2):
        shape = x.shape
        D = shape[-1]
        y, dx, hs, gs, us, dzs, _ = _run_pass(x.reshape(-1, D), g.reshape(-1, D), w1[0], w2[0])
        y, dx, dw1, dw2 = _run_grads(hs, gs, us, dzs, y, dx)
        return y.reshape(shape), dx.reshape(shape), dw1[None], dw2[None]

    return jax.shard_map(body, mesh=mesh,
                         in_specs=(P('data'), P('data'), P('stage'), P('stage')),
                         out_specs=(P('data'), P('data'), P(('data', 'stage')), P(('data', 'stage'))),
                         check_vma=False)
```

time: 430 us -> 404 us (0.940)
  matrix products: 93.3 us -> 0 us
  Pallas kernels: 327 us -> 401 us
  local copies, waits for them, and re-layouts: 5.43 us -> 0 us
    dot_general x2 -> x0, matrix products: 93.3 us -> none  [_dot_k0(): lax.dot_general(a, b, (((0,), (0,)), ((), ())), preferred_element_type=F32)]
    pallas_call x1 -> x2, Pallas kernels: 327 us -> 401 us  [the longest x1 307 us: _run_pass(): pl.pallas_call(functools.partial(_pass_kernel, C, T, NT), out_shape=(act,...]
    unnamed x12 -> x0, local copies, waits for them, and re-layouts: 5.43 us -> none
where the time goes in v2:
time: 404 us; the launch traced here: 402 us
  Pallas kernels  401 us (99%)
    pallas_call x1, Pallas kernels, _run_pass(): pl.pallas_call(functools.partial(_pass_kernel, C, T, NT), out_shape=(act,...  307 us
    pallas_call x1, Pallas kernels, _run_grads(): pl.pallas_call(functools.partial(_grad_kernel, n1), grid=(2 * n1,), in_sp...  94.3 us

profile of v2, /device:TPU:0, one launch (start us, length us, event | category | flops | bytes accessed | tf_op | source)
XLA Modules:
  0.0 401.7 jit_solution(14141119832188302451)
XLA Ops:
  0.6 306.6 %mlp_pass.1 = (bf16[2048,1536]{1,0:T(8,128)(2,1)}, bf16[2048,1536]{1,0:T(8,128)(2,1)}, bf16[2048,1536]{1,0:T(8,128)(2,1)}, bf16[2048,1536]{1,0:T(8,128)(2,1)}, b...) custom-call(bf16[2048,1536]{1,0:T(8,128)(2,1)} %bitcast.10, ...), custom_call_target="tpu_custom_call" | custom-call | tf_op jit(solution)/shard_map/mlp_pass/pallas_call | solution.py:394
  307.2 94.3 %mlp_grads.1 = (bf16[2048,1536]{1,0:T(8,128)(2,1)}, bf16[2048,1536]{1,0:T(8,128)(2,1)}, f32[1536,6144]{1,0:T(8,128)}, f32[6144,1536]{1,0:T(8,128)}) custom-call(bf16[2048,1536]{1,0:T(8,128)(2,1)} %get-tuple-element.14.x_any, bf16[2048,1536]{1,0:T(8,128)(2,1)} %get-tuple-element.15.g_any, bf16[2048,1536]{1,0:T(8,128)(2,1)} %get-tuple-element.16.yi, ...), custom_call_target="tpu_custom_call" | custom-call | flops 77309411328 | bytes 209715200 | tf_op jit(solution)/shard_map/mlp_grads/pallas_call | solution.py:454
